TPU v7x, 32 devices: a whole 2x2x4 slice. The times are simulated.
32 devices in a mesh: row: 8 (over z, core), col: 4 (over y, x).
Axes of the slice: x: 2, y: 2, z: 4, core: 2. Of those that a mesh axis runs over, the one named last changes fastest.
Arguments:
- x_fwd: bfloat16 [512, 6144], P('row', 'col'), may hold values from -6 to 6
- x_bwd: bfloat16 [512, 6144], P('row', 'col'), may hold values from -6 to 6
- grad_out: bfloat16 [512, 6144], P('row', 'col'), may hold values from -1.5 to 1.5
- gain: float32 [6144], P('col'), may hold values from 0.1 to 1.9
- w_up: bfloat16 [6144, 12288], P('col', 'row'), may hold values from -0.078125 to 0.078125
- w_down: bfloat16 [12288, 6144], P('row', 'col'), may hold values from -0.0546875 to 0.0546875
Outputs:
- y_fwd: bfloat16 [512, 6144], P('row', 'col')
- dx_bwd: bfloat16 [512, 6144], P('row', 'col')
- step_up: float32 [6144, 12288], P('col', 'row')
- step_down: float32 [12288, 6144], P('row', 'col')
- step_gain: float32 [6144], P('col')
- grad_rms: float32 [], replicated
All inputs are finite; a program needn't handle non-finite values.
Results may differ from a plain program's by a relative error of at most 0.0017.
The roundings to bfloat16 on the way count: a program that leaves them out, or rounds other values in their place, can miss the bound.
Values may be sent and summed in bfloat16 or wider, within the bound.
A program may use at most 128 MiB of HBM per device.

v0:
```python
import math
import jax
import jax.numpy as jnp
from jax import lax
from jax.sharding import PartitionSpec as P

D = 6144
FF = 12288
eps = 1e-06
clip_share = 0.25


def erf_gelu(value):
    return 0.5 * value * (1.0 + lax.erf(value * 0.7071067811865476))


def gelu_slope(value):
    return (
        0.5 * (1.0 + lax.erf(value * 0.7071067811865476))
        + value * jnp.exp(-0.5 * value * value) * 0.3989422804014327
    )


def contract(left, right, left_dim, right_dim):
    return lax.dot_general(
        left, right, (((left_dim,), (right_dim,)), ((), ())), preferred_element_type=jnp.float32
    )


def row_sums(tokens):
    values = tokens.astype(jnp.float32)
    return (jnp.sum(values, -1), jnp.sum(values * values, -1))


def normalize(tokens, first, second):
    values = tokens.astype(jnp.float32)
    centre = first / D
    spread = second / D - centre * centre
    inv_scale = lax.rsqrt(spread + eps)
    return ((values - centre[:, None]) * inv_scale[:, None], inv_scale)


def up_both(normed_a, normed_b, w_up):
    full_a, full_b = (
        lax.all_gather(normed_a, "row", axis=0, tiled=True),
        lax.all_gather(normed_b, "row", axis=0, tiled=True),
    )
    width = w_up.shape[1]
    summed = lax.psum_scatter(
        jnp.concatenate(
            [
                jnp.dot(full_a, w_up, preferred_element_type=jnp.float32),
                jnp.dot(full_b, w_up, preferred_element_type=jnp.float32),
            ],
            1,
        ),
        "col",
        scatter_dimension=0,
        tiled=True,
    )
    return (summed[:, :width], summed[:, width:], full_b)


def on_device(x_fwd, x_bwd, grad_out, gain, w_up, w_down):
    first_a, second_a = row_sums(x_fwd)
    first_b, second_b = row_sums(x_bwd)
    first_a, second_a, first_b, second_b = lax.psum((first_a, second_a, first_b, second_b), "col")
    centred_a, _ = normalize(x_fwd, first_a, second_a)
    centred_b, inv_scale = normalize(x_bwd, first_b, second_b)
    normed_a = (centred_a * gain).astype(jnp.bfloat16)
    normed_b = (centred_b * gain).astype(jnp.bfloat16)
    pre_a, pre_b, normed_full = up_both(normed_a, normed_b, w_up)
    hidden_a = erf_gelu(pre_a).astype(jnp.bfloat16)
    output_part = jnp.dot(
        lax.all_gather(hidden_a, "col", axis=0, tiled=True),
        w_down,
        preferred_element_type=jnp.float32,
    )
    output_sum = lax.psum_scatter(output_part, "row", scatter_dimension=0, tiled=True)
    y_fwd = (x_fwd.astype(jnp.float32) + output_sum).astype(jnp.bfloat16)
    hidden_b = erf_gelu(pre_b).astype(jnp.bfloat16)
    grad_full = lax.all_gather(grad_out, "row", axis=0, tiled=True)
    grad_hidden = lax.psum_scatter(
        contract(grad_full, w_down, 1, 1), "col", scatter_dimension=0, tiled=True
    )
    grad_pre = (grad_hidden * gelu_slope(pre_b)).astype(jnp.bfloat16)
    hidden_piece = lax.all_gather(hidden_b, "col", axis=0, tiled=True)
    pre_piece = lax.all_gather(grad_pre, "col", axis=0, tiled=True)
    down_total = contract(hidden_piece, grad_full, 0, 0)
    up_total = contract(normed_full, pre_piece, 0, 0)
    input_total = contract(pre_piece, w_up, 1, 1)
    grad_normed = lax.psum_scatter(input_total, "row", scatter_dimension=0, tiled=True)
    scaled = grad_normed * gain
    first_back = jnp.sum(scaled, -1)
    second_back = jnp.sum(scaled * centred_b, -1)
    first_back, second_back = lax.psum((first_back, second_back), "col")
    dx_bwd = (
        grad_out.astype(jnp.float32)
        + inv_scale[:, None]
        * (scaled - first_back[:, None] / D - centred_b * (second_back[:, None] / D))
    ).astype(jnp.bfloat16)
    gain_part = jnp.sum(grad_normed * centred_b, 0)
    weight_squares = jnp.sum(up_total * up_total) + jnp.sum(down_total * down_total)
    g_gain = lax.psum(gain_part, "row")
    first_row = (lax.axis_index("row") == 0).astype(jnp.float32)
    total = lax.psum(weight_squares + first_row * jnp.sum(g_gain * g_gain), ("row", "col"))
    param_count = 2 * D * FF + D
    norm_value = jnp.sqrt(total)
    grad_rms = norm_value / math.sqrt(param_count)
    factor = jnp.minimum(1.0, clip_share * math.sqrt(param_count) / norm_value)
    return (y_fwd, dx_bwd, up_total * factor, down_total * factor, g_gain * factor, grad_rms)


def solution(mesh):
    placed = (
        P("row", "col"),
        P("row", "col"),
        P("row", "col"),
        P("col"),
        P("col", "row"),
        P("row", "col"),
    )
    return jax.shard_map(
        on_device,
        mesh=mesh,
        in_specs=placed,
        out_specs=(
            P("row", "col"),
            P("row", "col"),
            P("col", "row"),
            P("row", "col"),
            P("col"),
            P(),
        ),
        check_vma=False,
    )
```

profile of v0, /device:TPU:0, one launch (start us, length us, event | category | flops | bytes accessed | tf_op | source)
XLA Modules:
  0.0 446.6 jit_solution(12459251885347289089)
XLA Ops:
  7.2 0.0 all-gather.13.cloned.1.call-start
  7.2 0.7 all-gather.13.cloned.1.call-update
  7.9 0.0 all-gather.7.cloned.1.call-start
  7.9 1.1 convert_reduce_fusion
  9.0 1.1 convert_reduce_fusion.1
  10.1 11.4 %all-reduce.1 = (f32[64]{0:T(128)S(1)}, f32[64]{0:T(128)S(1)}, f32[64]{0:T(128)S(1)}, f32[64]{0:T(128)S(1)}) all-reduce(f32[64]{0:T(128)S(1)} %get-tuple-element.12, f32[64]{0:T(128)S(1)} %get-tuple-element.11, f32[64]{0:T(128)S(1)} %get-tuple-element.10, f32[64]{0:T(128)S(1)} %get-tuple-element.9), channel_id=1, replica_groups=mesh['row'=8,'col'=4] {'col'}, use_global_device_ids=true, to_apply=%region_7.0 | all-reduce | flops 256 | bytes 2048 | tf_op jit(solution)/shard_map/psum | solution.py:67
  21.5 2.0 fusion.21
  23.6 0.0 all-gather.7.cloned.1.call-update
  23.6 0.0 all-gather.9.cloned.1.call-start
  23.6 0.7 all-gather.9.cloned.1.call-update
  24.3 0.0 reduce-scatter.9.cloned.1.call-start
  24.4 13.3 %all-gather.13.cloned.1.call-done = bf16[512,1536]{1,0:T(8,128)(2,1)} async-done(((bf16[64,1536]{1,0:T(8,128)(2,1)}), bf16[512,1536]{1,0:T(8,128)(2,1)}) %all-gather.13.cloned.1.call-update) | async-done | bytes 1572880 | tf_op jit(solution)/shard_map/all_gather | solution.py:82
  37.6 7.1 %fusion.27 = f32[512,1536]{1,0:T(8,128)} fusion(bf16[512,1536]{1,0:T(8,128)(2,1)} %all-gather.13.cloned.1.call-done, bf16[1536,1536]{1,0:T(8,128)(2,1)} %param.11), kind=kOutput, calls=%fused_computation.52 | convolution fusion | flops 2415919104 | bytes 9437184 | tf_op jit(solution)/shard_map/dot_general | solution.py:25
  44.8 0.0 reduce-scatter.9.cloned.1.call-update
  44.8 0.0 reduce-scatter.5.cloned.1.call-start
  44.8 19.4 %all-gather.7.cloned.1.call-done = bf16[512,1536]{1,0:T(8,128)(2,1)} async-done(((bf16[64,1536]{1,0:T(8,128)(2,1)}), bf16[512,1536]{1,0:T(8,128)(2,1)}) %all-gather.7.cloned.1.call-update) | async-done | bytes 1572880 | tf_op jit(solution)/shard_map/all_gather | solution.py:45
  64.3 4.9 %fusion.24 = f32[512,1536]{1,0:T(8,128)S(1)} fusion(bf16[512,1536]{1,0:T(8,128)(2,1)} %all-gather.7.cloned.1.call-done, bf16[1536,1536]{1,0:T(8,128)(2,1)} %param.10), kind=kOutput, calls=%fused_computation.49 | convolution fusion | flops 2415919104 | bytes 9437184 | tf_op jit(solution)/shard_map/dot_general | solution.py:52
  69.2 21.7 %all-gather.9.cloned.1.call-done = bf16[512,1536]{1,0:T(8,128)(2,1)} async-done(((bf16[64,1536]{1,0:T(8,128)(2,1)}), bf16[512,1536]{1,0:T(8,128)(2,1)}) %all-gather.9.cloned.1.call-update) | async-done | bytes 1572880 | tf_op jit(solution)/shard_map/all_gather | solution.py:46
  90.9 4.9 %fusion.25 = f32[512,1536]{1,0:T(8,128)S(1)} fusion(bf16[512,1536]{1,0:T(8,128)(2,1)} %all-gather.9.cloned.1.call-done, bf16[1536,1536]{1,0:T(8,128)(2,1)} %param.10), kind=kOutput, calls=%fused_computation.50 | convolution fusion | flops 2415919104 | bytes 9437184 | tf_op jit(solution)/shard_map/dot_general | solution.py:53
  95.9 3.3 pad_maximum_fusion
  99.1 0.0 reduce-scatter.5.cloned.1.call-update
  99.1 0.0 all-gather.15.cloned.1.call-start
  99.2 38.2 %reduce-scatter.9.cloned.1.call-done = f32[128,1536]{1,0:T(8,128)} async-done(((f32[512,1536]{1,0:T(8,128)}), f32[128,1536]{1,0:T(8,128)}) %reduce-scatter.9.cloned.1.call-update) | async-done | bytes 786448 | tf_op jit(solution)/shard_map/reduce_scatter | solution.py:83
  137.4 73.5 %reduce-scatter.5.cloned.1.call-done = f32[128,3072]{1,0:T(8,128)} async-done(((f32[512,3072]{1,0:T(8,128)}), f32[128,3072]{1,0:T(8,128)}) %reduce-scatter.5.cloned.1.call-update) | async-done | bytes 1572880 | tf_op jit(solution)/shard_map/reduce_scatter | solution.py:49
  210.9 3.0 multiply_convert_fusion
  213.9 0.0 all-gather.15.cloned.1.call-update
  213.9 0.0 all-gather.11.cloned.1.call-start
  214.0 0.7 all-gather.11.cloned.1.call-update
  214.7 0.0 all-gather.17.cloned.1.call-start
  214.7 0.7 all-gather.17.cloned.1.call-update
  215.4 0.0 reduce-scatter.11.cloned.1.call-start
  215.5 29.5 %all-gather.15.cloned.1.call-done = bf16[512,1536]{1,0:T(8,128)(2,1)} async-done(((bf16[128,1536]{1,0:T(8,128)(2,1)}), bf16[512,1536]{1,0:T(8,128)(2,1)}) %all-gather.15.cloned.1.call-update) | async-done | bytes 1572880 | tf_op jit(solution)/shard_map/all_gather | solution.py:88
  244.9 7.1 %fusion.28 = f32[512,1536]{1,0:T(8,128)} fusion(bf16[512,1536]{1,0:T(8,128)(2,1)} %all-gather.15.cloned.1.call-done, bf16[1536,1536]{1,0:T(8,128)(2,1)} %param.10), kind=kOutput, calls=%fused_computation.53 | convolution fusion | flops 2415919104 | bytes 9437184 | tf_op jit(solution)/shard_map/dot_general | solution.py:25
  252.0 0.0 reduce-scatter.11.cloned.1.call-update
  252.1 0.2 reduce-scatter.7.cloned.1.call-start
  252.3 25.3 %all-gather.11.cloned.1.call-done = bf16[512,1536]{1,0:T(8,128)(2,1)} async-done(((bf16[128,1536]{1,0:T(8,128)(2,1)}), bf16[512,1536]{1,0:T(8,128)(2,1)}) %all-gather.11.cloned.1.call-update) | async-done | bytes 1572880 | tf_op jit(solution)/shard_map/all_gather | solution.py:75
  277.6 7.1 %fusion.26 = f32[512,1536]{1,0:T(8,128)} fusion(bf16[512,1536]{1,0:T(8,128)(2,1)} %all-gather.11.cloned.1.call-done, bf16[1536,1536]{1,0:T(8,128)(2,1)} %param.11), kind=kOutput, calls=%fused_computation.51 | convolution fusion | flops 2415919104 | bytes 9437184 | tf_op jit(solution)/shard_map/dot_general | solution.py:74
  284.8 0.0 reduce-scatter.7.cloned.1.call-update
  284.8 1.4 copy-done.5
  286.2 0.5 copy-done.6
  286.7 6.0 %multiply_reduce_fusion.1 = (f32[]{:T(128)}, f32[1536,1536]{1,0:T(8,128)}) fusion(bf16[512,1536]{1,0:T(8,128)(2,1)S(1)} %copy-done.5, bf16[512,1536]{1,0:T(8,128)(2,1)S(1)} %copy-done.6), kind=kOutput, calls=%fused_computation.1 | convolution fusion | flops 2420637696 | bytes 12582916 | tf_op jit(solution)/shard_map/dot_general | solution.py:25
  292.7 18.2 %all-gather.17.cloned.1.call-done = bf16[512,1536]{1,0:T(8,128)(2,1)} async-done(((bf16[128,1536]{1,0:T(8,128)(2,1)}), bf16[512,1536]{1,0:T(8,128)(2,1)}) %all-gather.17.cloned.1.call-update) | async-done | bytes 1572880 | tf_op jit(solution)/shard_map/all_gather | solution.py:87
  310.9 8.9 %multiply_reduce_fusion = (f32[]{:T(128)}, f32[1536,1536]{1,0:T(8,128)}) fusion(bf16[512,1536]{1,0:T(8,128)(2,1)} %all-gather.17.cloned.1.call-done, bf16[512,1536]{1,0:T(8,128)(2,1)} %all-gather.13.cloned.1.call-done), kind=kOutput, calls=%fused_computation | convolution fusion | flops 2420637696 | bytes 12582916 | tf_op jit(solution)/shard_map/dot_general | solution.py:25
  321.1 32.5 %reduce-scatter.11.cloned.1.call-done = f32[64,1536]{1,0:T(8,128)} async-done(((f32[512,1536]{1,0:T(8,128)}), f32[64,1536]{1,0:T(8,128)}) %reduce-scatter.11.cloned.1.call-update) | async-done | bytes 393232 | tf_op jit(solution)/shard_map/reduce_scatter | solution.py:92
  353.6 0.0 copy-done
  353.6 0.0 copy-done.4
  353.6 1.4 fusion.17
  355.0 16.1 %psum.62 = f32[1536]{0:T(1024)S(1)} all-reduce(f32[1536]{0:T(1024)S(1)} %get-tuple-element.6), channel_id=1, replica_groups=mesh['row'=8,'col'=4] {'row'}, use_global_device_ids=true, to_apply=%region_19.0 | all-reduce | flops 1536 | bytes 12288 | tf_op jit(solution)/shard_map/psum | solution.py:104
  371.1 0.6 multiply_reduce_fusion.3
  372.3 38.8 %psum.63 = f32[]{:T(128)} all-reduce(f32[]{:T(128)S(6)} %add.60), channel_id=1, replica_groups=mesh['row'=8,'col'=4] {'row','col'}, use_global_device_ids=true, to_apply=%region_21.0 | all-reduce | flops 1 | bytes 8 | tf_op jit(solution)/shard_map/psum | solution.py:106
  411.9 9.9 %all-reduce = (f32[64]{0:T(128)S(1)}, f32[64]{0:T(128)S(1)}) all-reduce(f32[64]{0:T(128)S(1)} %get-tuple-element.7, f32[64]{0:T(128)S(1)} %get-tuple-element.8), channel_id=1, replica_groups=mesh['row'=8,'col'=4] {'col'}, use_global_device_ids=true, to_apply=%region_15.0 | all-reduce | flops 128 | bytes 1024 | tf_op jit(solution)/shard_map/psum | solution.py:96
  421.8 0.6 broadcast_multiply_fusion.2
  422.5 8.7 %broadcast_multiply_fusion = f32[1536,1536]{1,0:T(8,128)} fusion(f32[1536,1536]{1,0:T(8,128)} %get-tuple-element.31, f32[]{:T(128)S(6)} %min.3), kind=kLoop, calls=%fused_computation.3 | loop fusion | flops 2359296 | bytes 18874372 | tf_op jit(solution)/shard_map/mul | solution.py:111
  431.1 0.0 slice-done
  431.1 0.0 slice-done.1
  431.1 0.0 slice-done.2
  431.1 0.0 copy-start.1
  431.2 0.0 copy-start.2
  431.2 0.0 copy-start.3
  431.2 4.8 %broadcast_multiply_fusion.1 = f32[1536,1536]{1,0:T(8,128)} fusion(f32[1536,1536]{1,0:T(8,128)S(1)} %bitcast.15, f32[]{:T(128)S(6)} %min.3), kind=kLoop, calls=%fused_computation.4 | loop fusion | flops 2359296 | bytes 18874372 | tf_op jit(solution)/shard_map/mul | solution.py:111
  436.0 0.0 copy-done.1
  436.0 1.7 fusion.23
  437.7 0.0 copy-done.3
  437.7 0.9 fusion.16
  (13 shorter events, 0.0 us)
Async XLA Ops:
  7.2 30.5 %all-gather.13.cloned.1.call-start = ((), (), s32[]{:S(2)}) async-start(), calls=%async_computation.9 | async-start | bytes 1769472 | tf_op jit(solution)/shard_map/all_gather | solution.py:82
  7.9 56.4 %all-gather.7.cloned.1.call-start = ((), (), s32[]{:S(2)}) async-start(), calls=%async_computation.4 | async-start | bytes 1769472 | tf_op jit(solution)/shard_map/all_gather | solution.py:45
  23.6 67.3 %all-gather.9.cloned.1.call-start = ((), (), s32[]{:S(2)}) async-start(), calls=%async_computation.5 | async-start | bytes 1769472 | tf_op jit(solution)/shard_map/all_gather | solution.py:46
  24.3 113.1 %reduce-scatter.9.cloned.1.call-start = ((), (), s32[]{:S(2)}) async-start(), calls=%async_computation.10 | async-start | bytes 3932160 | tf_op jit(solution)/shard_map/reduce_scatter | solution.py:83
  44.8 166.1 %reduce-scatter.5.cloned.1.call-start = ((), (), s32[]{:S(2)}) async-start(), calls=%async_computation.6 | async-start | bytes 7864320 | tf_op jit(solution)/shard_map/reduce_scatter | solution.py:49
  99.1 145.8 %all-gather.15.cloned.1.call-start = ((), (), s32[]{:S(2)}) async-start(), calls=%async_computation.11 | async-start | bytes 1966080 | tf_op jit(solution)/shard_map/all_gather | solution.py:88
  213.9 63.7 %all-gather.11.cloned.1.call-start = ((), (), s32[]{:S(2)}) async-start(), calls=%async_computation.7 | async-start | bytes 1966080 | tf_op jit(solution)/shard_map/all_gather | solution.py:75
  214.7 96.2 %all-gather.17.cloned.1.call-start = ((), (), s32[]{:S(2)}) async-start(), calls=%async_computation.13 | async-start | bytes 1966080 | tf_op jit(solution)/shard_map/all_gather | solution.py:87
  215.4 138.2 %reduce-scatter.11.cloned.1.call-start = ((), (), s32[]{:S(2)}) async-start(), calls=%async_computation.12 | async-start | bytes 3538944 | tf_op jit(solution)/shard_map/reduce_scatter | solution.py:92
  252.1 183.9 %reduce-scatter.7.cloned.1.call-start = ((), (), s32[]{:S(2)}) async-start(), calls=%async_computation.8 | async-start | bytes 3538944 | tf_op jit(solution)/shard_map/reduce_scatter | solution.py:79
  284.8 1.4 copy-start.5
  284.8 1.9 copy-start.6
  292.7 60.9 %copy-start = (bf16[64,1536]{1,0:T(8,128)(2,1)S(1)}, bf16[64,1536]{1,0:T(8,128)(2,1)}, u32[]{:S(2)}) copy-start(bf16[64,1536]{1,0:T(8,128)(2,1)} %param.7) | copy-start | bytes 589828
  292.7 60.9 %copy-start.4 = (f32[1536]{0:T(1024)S(1)}, f32[1536]{0:T(1024)}, u32[]{:S(2)}) copy-start(f32[1536]{0:T(1024)} %param.9) | copy-start | bytes 18436
  353.6 77.5 %slice-start = ((s8[9437184]{0:T(1024)(128)(4,1)}), s8[1048576]{0:T(1024)(128)(4,1)S(1)}, s32[]{:S(2)}) async-start(s8[9437184]{0:T(1024)(128)(4,1)} %bitcast.14), calls=%async_computation.14 | async-start | bytes 2097152
  422.4 8.7 %slice-start.1 = ((s8[9437184]{0:T(1024)(128)(4,1)}), s8[4194304]{0:T(1024)(128)(4,1)S(1)}, s32[]{:S(2)}) async-start(s8[9437184]{0:T(1024)(128)(4,1)} %bitcast.14), calls=%async_computation.15 | async-start | bytes 8388608
  422.4 8.7 %slice-start.2 = ((s8[9437184]{0:T(1024)(128)(4,1)}), s8[4194304]{0:T(1024)(128)(4,1)S(1)}, s32[]{:S(2)}) async-start(s8[9437184]{0:T(1024)(128)(4,1)} %bitcast.14), calls=%async_computation.16 | async-start | bytes 8388608
  431.1 4.8 %copy-start.1 = (bf16[64,1536]{1,0:T(8,128)(2,1)S(1)}, bf16[64,1536]{1,0:T(8,128)(2,1)}, u32[]{:S(2)}) copy-start(bf16[64,1536]{1,0:T(8,128)(2,1)} %param.6) | copy-start | bytes 589828
  431.2 6.5 %copy-start.2 = (f32[64,1536]{1,0:T(8,128)S(1)}, f32[64,1536]{1,0:T(8,128)}, u32[]{:S(2)}) copy-start(f32[64,1536]{1,0:T(8,128)} %reduce-scatter.11.cloned.1.call-done) | copy-start | bytes 1179652
  431.2 6.5 %copy-start.3 = (bf16[64,1536]{1,0:T(8,128)(2,1)S(1)}, bf16[64,1536]{1,0:T(8,128)(2,1)}, u32[]{:S(2)}) copy-start(bf16[64,1536]{1,0:T(8,128)(2,1)} %param.8) | copy-start | bytes 589828
Sparse Core Ops, SparseCore 0:
  9.6 27.9 all-gather.12
  39.8 24.3 all-gather.6
  66.5 24.3 all-gather.8
  94.3 43.0 reduce-scatter.8
  140.8 70.0 reduce-scatter.4
  214.0 30.8 all-gather.14
  246.8 30.8 all-gather.10
  280.0 30.8 all-gather.16
  313.2 40.3 reduce-scatter.10
  355.8 40.2 reduce-scatter.6
where the time goes:
time: 447 us
  waiting for transfers between devices  274 us (61%)
  blocking collectives  76.2 us (17%)
  matrix products  46.1 us (10%)
  other arithmetic  29.2 us (7%)
  between operations  18.1 us (4%)
    reduce_scatter x1, waiting for transfers between devices, up_both(): lax.psum_scatter(jnp.concatenate([jnp.dot(full_a, w_up, preferred_element...  73.5 us
    psum x1, blocking collectives, on_device(): lax.psum(weight_squares + first_row * jnp.sum(g_gain * g_gain), ('row', '...  38.8 us
    reduce_scatter x1, waiting for transfers between devices, on_device(): lax.psum_scatter(contract(grad_full, w_down, 1, 1), 'col', scatter_dimens...  38.2 us
    reduce_scatter x1, waiting for transfers between devices, on_device(): lax.psum_scatter(input_total, 'row', scatter_dimension=0, tiled=True)  32.5 us
    all_gather x1, waiting for transfers between devices, on_device(): pre_piece = lax.all_gather(grad_pre, 'col', axis=0, tiled=True)  29.5 us
    dot_general x4, matrix products, contract(): lax.dot_general(left, right, (((left_dim,), (right_dim,)), ((), ())), pre...  29.2 us
    all_gather x1, waiting for transfers between devices, on_device(): lax.all_gather(hidden_a, 'col', axis=0, tiled=True)  25.3 us
    all_gather x1, waiting for transfers between devices, up_both(): lax.all_gather(normed_b, 'row', axis=0, tiled=True)  21.7 us
  transfers between devices with their start and end apart: 10, of which 9 were waited for; matrix products, arithmetic and copies ran while one was open for 16% of the time, Pallas kernels for 0%

commit v1 on v0

--- a/solution.py
+++ b/solution.py
@@ -8,6 +8,16 @@
 FF = 12288
 eps = 1e-06
 clip_share = 0.25
+
+
+def turned_line(value, axis, dim):
+    peers = lax.axis_size(axis)
+    moving, tiles = (value, [value])
+    for _ in range(peers - 1):
+        moving = lax.ppermute(moving, axis, [(i, (i + 1) % peers) for i in range(peers)])
+        tiles.insert(0, moving)
+    flat = jnp.concatenate(tiles, axis=dim)
+    return jnp.roll(flat, (lax.axis_index(axis) + 1) * value.shape[dim], axis=dim)
 
 
 def erf_gelu(value):
@@ -85,7 +95,7 @@
     )
     grad_pre = (grad_hidden * gelu_slope(pre_b)).astype(jnp.bfloat16)
     hidden_piece = lax.all_gather(hidden_b, "col", axis=0, tiled=True)
-    pre_piece = lax.all_gather(grad_pre, "col", axis=0, tiled=True)
+    pre_piece = turned_line(grad_pre, "col", 0)
     down_total = contract(hidden_piece, grad_full, 0, 0)
     up_total = contract(normed_full, pre_piece, 0, 0)
     input_total = contract(pre_piece, w_up, 1, 1)

time: 447 us -> 424 us (0.949)
  waiting for transfers between devices: 274 us -> 243 us
  starting transfers between devices: 0.58 us -> 5.42 us
    ppermute x0 -> x3, waiting for transfers between devices: none -> 37.2 us  [turned_line(): lax.ppermute(moving, axis, [(i, (i + 1) % peers) for i in range(peers)])]
    all_gather x1 -> x0, waiting for transfers between devices: 29.5 us -> none  [on_device(): pre_piece = lax.all_gather(grad_pre, 'col', axis=0, tiled=True)]
    all_gather x1, waiting for transfers between devices: 25.3 us -> 0.02 us  [on_device(): lax.all_gather(hidden_a, 'col', axis=0, tiled=True)]
    all_gather x1, waiting for transfers between devices: 18.2 us -> 5.23 us  [on_device(): hidden_piece = lax.all_gather(hidden_b, 'col', axis=0, tiled=True)]
    ppermute x0 -> x3, starting transfers between devices: none -> 4.87 us  [turned_line(): lax.ppermute(moving, axis, [(i, (i + 1) % peers) for i in range(peers)])]
  transfers between devices with their start and end apart: 10 -> 12, of which waited for: 9 -> 10; matrix products, arithmetic and copies ran while one was open for 16% -> 17% of each run, Pallas kernels for 0% -> 0%
where the time goes in v1:
time: 424 us; the launch traced here: 423 us
  waiting for transfers between devices  243 us (57%)
  blocking collectives  76.2 us (18%)
  matrix products  47.1 us (11%)
  other arithmetic  30.2 us (7%)
  between operations  17.8 us (4%)
  starting transfers between devices  5.42 us (1%)
    reduce_scatter x1, waiting for transfers between devices, up_both(): lax.psum_scatter(jnp.concatenate([jnp.dot(full_a, w_up, preferred_element...  73.5 us
    psum x1, blocking collectives, on_device(): lax.psum(weight_squares + first_row * jnp.sum(g_gain * g_gain), ('row', '...  38.5 us
    reduce_scatter x1, waiting for transfers between devices, on_device(): lax.psum_scatter(contract(grad_full, w_down, 1, 1), 'col', scatter_dimens...  38.2 us
    ppermute x3, waiting for transfers between devices, turned_line(): lax.ppermute(moving, axis, [(i, (i + 1) % peers) for i in range(peers)])  37.2 us
    reduce_scatter x1, waiting for transfers between devices, on_device(): lax.psum_scatter(input_total, 'row', scatter_dimension=0, tiled=True)  32.5 us
    dot_general x4, matrix products, contract(): lax.dot_general(left, right, (((left_dim,), (right_dim,)), ((), ())), pre...  30.1 us
    all_gather x1, waiting for transfers between devices, up_both(): lax.all_gather(normed_b, 'row', axis=0, tiled=True)  21.7 us
    all_gather x1, waiting for transfers between devices, up_both(): lax.all_gather(normed_a, 'row', axis=0, tiled=True)  19.4 us
  transfers between devices with their start and end apart: 12, of which 10 were waited for; matrix products, arithmetic and copies ran while one was open for 17% of the time, Pallas kernels for 0%

profile of v1, /device:TPU:0, one launch (start us, length us, event | category | flops | bytes accessed | tf_op | source)
XLA Modules:
  0.0 423.0 jit_solution(10006739307052160839)
XLA Ops:
  7.2 0.0 all-gather.12.cloned.1.call-start
  7.2 0.7 all-gather.12.cloned.1.call-update
  7.9 0.0 all-gather.6.cloned.1.call-start
  7.9 1.1 convert_reduce_fusion
  9.0 1.1 convert_reduce_fusion.1
  10.1 11.4 %all-reduce.1 = (f32[64]{0:T(128)S(1)}, f32[64]{0:T(128)S(1)}, f32[64]{0:T(128)S(1)}, f32[64]{0:T(128)S(1)}) all-reduce(f32[64]{0:T(128)S(1)} %get-tuple-element.12, f32[64]{0:T(128)S(1)} %get-tuple-element.11, f32[64]{0:T(128)S(1)} %get-tuple-element.10, f32[64]{0:T(128)S(1)} %get-tuple-element.9), channel_id=1, replica_groups=mesh['row'=8,'col'=4] {'col'}, use_global_device_ids=true, to_apply=%region_7.0 | all-reduce | flops 256 | bytes 2048 | tf_op jit(solution)/shard_map/psum | solution.py:77
  21.5 2.0 fusion.25
  23.6 0.0 all-gather.6.cloned.1.call-update
  23.6 0.0 all-gather.8.cloned.1.call-start
  23.6 0.7 all-gather.8.cloned.1.call-update
  24.3 0.0 reduce-scatter.9.cloned.1.call-start
  24.4 13.3 %all-gather.12.cloned.1.call-done = bf16[512,1536]{1,0:T(8,128)(2,1)} async-done(((bf16[64,1536]{1,0:T(8,128)(2,1)}), bf16[512,1536]{1,0:T(8,128)(2,1)}) %all-gather.12.cloned.1.call-update) | async-done | bytes 1572880 | tf_op jit(solution)/shard_map/all_gather | solution.py:92
  37.6 7.1 %fusion.33 = f32[512,1536]{1,0:T(8,128)} fusion(bf16[512,1536]{1,0:T(8,128)(2,1)} %all-gather.12.cloned.1.call-done, bf16[1536,1536]{1,0:T(8,128)(2,1)} %param.11), kind=kOutput, calls=%fused_computation.66 | convolution fusion | flops 2415919104 | bytes 9437184 | tf_op jit(solution)/shard_map/dot_general | solution.py:35
  44.8 0.0 reduce-scatter.9.cloned.1.call-update
  44.8 0.0 reduce-scatter.5.cloned.1.call-start
  44.8 19.4 %all-gather.6.cloned.1.call-done = bf16[512,1536]{1,0:T(8,128)(2,1)} async-done(((bf16[64,1536]{1,0:T(8,128)(2,1)}), bf16[512,1536]{1,0:T(8,128)(2,1)}) %all-gather.6.cloned.1.call-update) | async-done | bytes 1572880 | tf_op jit(solution)/shard_map/all_gather | solution.py:55
  64.3 4.9 %fusion.30 = f32[512,1536]{1,0:T(8,128)S(1)} fusion(bf16[512,1536]{1,0:T(8,128)(2,1)} %all-gather.6.cloned.1.call-done, bf16[1536,1536]{1,0:T(8,128)(2,1)} %param.10), kind=kOutput, calls=%fused_computation.63 | convolution fusion | flops 2415919104 | bytes 9437184 | tf_op jit(solution)/shard_map/dot_general | solution.py:62
  69.2 21.7 %all-gather.8.cloned.1.call-done = bf16[512,1536]{1,0:T(8,128)(2,1)} async-done(((bf16[64,1536]{1,0:T(8,128)(2,1)}), bf16[512,1536]{1,0:T(8,128)(2,1)}) %all-gather.8.cloned.1.call-update) | async-done | bytes 1572880 | tf_op jit(solution)/shard_map/all_gather | solution.py:56
  90.9 4.9 %fusion.31 = f32[512,1536]{1,0:T(8,128)S(1)} fusion(bf16[512,1536]{1,0:T(8,128)(2,1)} %all-gather.8.cloned.1.call-done, bf16[1536,1536]{1,0:T(8,128)(2,1)} %param.10), kind=kOutput, calls=%fused_computation.64 | convolution fusion | flops 2415919104 | bytes 9437184 | tf_op jit(solution)/shard_map/dot_general | solution.py:63
  95.9 3.3 pad_maximum_fusion
  99.1 0.0 reduce-scatter.5.cloned.1.call-update
  99.1 0.0 all-gather.10.cloned.1.call-start
  99.2 38.2 %reduce-scatter.9.cloned.1.call-done = f32[128,1536]{1,0:T(8,128)} async-done(((f32[512,1536]{1,0:T(8,128)}), f32[128,1536]{1,0:T(8,128)}) %reduce-scatter.9.cloned.1.call-update) | async-done | bytes 786448 | tf_op jit(solution)/shard_map/reduce_scatter | solution.py:93
  137.4 73.5 %reduce-scatter.5.cloned.1.call-done = f32[128,3072]{1,0:T(8,128)} async-done(((f32[512,3072]{1,0:T(8,128)}), f32[128,3072]{1,0:T(8,128)}) %reduce-scatter.5.cloned.1.call-update) | async-done | bytes 1572880 | tf_op jit(solution)/shard_map/reduce_scatter | solution.py:59
  210.9 3.0 multiply_convert_fusion
  213.9 0.0 all-gather.10.cloned.1.call-update
  213.9 0.0 all-gather.14.cloned.1.call-start
  213.9 1.5 collective-permute-start
  215.5 11.5 %collective-permute-done = bf16[128,1536]{1,0:T(8,128)(2,1)S(1)} collective-permute-done((bf16[128,1536]{1,0:T(8,128)(2,1)S(1)}, bf16[128,1536]{1,0:T(8,128)(2,1)S(1)}, u32[]{:S(2)}, u32[]{:S(2)}) %collective-permute-start) | collective-permute-done | bytes 393248 | tf_op jit(solution)/shard_map/ppermute | solution.py:17
  227.0 2.5 collective-permute-start.1
  229.5 8.8 %collective-permute-done.1 = bf16[128,1536]{1,0:T(8,128)(2,1)S(1)} collective-permute-done((bf16[128,1536]{1,0:T(8,128)(2,1)S(1)}, bf16[128,1536]{1,0:T(8,128)(2,1)S(1)}, u32[]{:S(2)}, u32[]{:S(2)}) %collective-permute-start.1) | collective-permute-done | bytes 393248 | tf_op jit(solution)/shard_map/ppermute | solution.py:17
  238.2 0.9 collective-permute-start.2
  239.1 0.0 all-gather.14.cloned.1.call-update
  239.1 0.0 reduce-scatter.11.cloned.1.call-start
  239.2 16.9 %collective-permute-done.2 = bf16[128,1536]{1,0:T(8,128)(2,1)S(1)} collective-permute-done((bf16[128,1536]{1,0:T(8,128)(2,1)S(1)}, bf16[128,1536]{1,0:T(8,128)(2,1)S(1)}, u32[]{:S(2)}, u32[]{:S(2)}) %collective-permute-start.2) | collective-permute-done | bytes 393248 | tf_op jit(solution)/shard_map/ppermute | solution.py:17
  256.3 0.0 copy-start.4
  256.4 1.7 copy-done.4
  258.0 6.7 %fusion.2 = f32[512,1536]{1,0:T(8,128)} fusion(bf16[1536,1536]{1,0:T(8,128)(2,1)} %param.10, bf16[1024,1536]{1,0:T(8,128)(2,1)S(1)} %constant_dynamic-update-slice_fusion, s32[]{:T(128)S(6)} %select_n.14), kind=kOutput, calls=%fused_computation.7 | convolution fusion | flops 2415919104 | bytes 9437188 | tf_op jit(solution)/shard_map/dot_general | solution.py:35
  264.7 0.0 reduce-scatter.11.cloned.1.call-update
  264.7 0.2 reduce-scatter.7.cloned.1.call-start
  265.0 0.0 all-gather.10.cloned.1.call-done
  265.0 7.1 %fusion.32 = f32[512,1536]{1,0:T(8,128)} fusion(bf16[512,1536]{1,0:T(8,128)(2,1)} %all-gather.10.cloned.1.call-done, bf16[1536,1536]{1,0:T(8,128)(2,1)} %param.11), kind=kOutput, calls=%fused_computation.65 | convolution fusion | flops 2415919104 | bytes 9437184 | tf_op jit(solution)/shard_map/dot_general | solution.py:84
  272.1 0.0 reduce-scatter.7.cloned.1.call-update
  272.1 1.9 copy-done.5
  274.0 7.5 %multiply_reduce_fusion.1 = (f32[]{:T(128)}, f32[1536,1536]{1,0:T(8,128)}) fusion(bf16[512,1536]{1,0:T(8,128)(2,1)} %all-gather.8.cloned.1.call-done, bf16[1024,1536]{1,0:T(8,128)(2,1)S(1)} %copy-done.5, s32[]{:T(128)S(6)} %select_n.14), kind=kOutput, calls=%fused_computation.1 | convolution fusion | flops 2420637696 | bytes 12582920 | tf_op jit(solution)/shard_map/dot_general | solution.py:35
  281.4 5.2 %all-gather.14.cloned.1.call-done = bf16[512,1536]{1,0:T(8,128)(2,1)} async-done(((bf16[128,1536]{1,0:T(8,128)(2,1)}), bf16[512,1536]{1,0:T(8,128)(2,1)}) %all-gather.14.cloned.1.call-update) | async-done | bytes 1572880 | tf_op jit(solution)/shard_map/all_gather | solution.py:97
  286.7 8.9 %multiply_reduce_fusion = (f32[]{:T(128)}, f32[1536,1536]{1,0:T(8,128)}) fusion(bf16[512,1536]{1,0:T(8,128)(2,1)} %all-gather.14.cloned.1.call-done, bf16[512,1536]{1,0:T(8,128)(2,1)} %all-gather.12.cloned.1.call-done), kind=kOutput, calls=%fused_computation | convolution fusion | flops 2420637696 | bytes 12582916 | tf_op jit(solution)/shard_map/dot_general | solution.py:35
  296.8 32.5 %reduce-scatter.11.cloned.1.call-done = f32[64,1536]{1,0:T(8,128)} async-done(((f32[512,1536]{1,0:T(8,128)}), f32[64,1536]{1,0:T(8,128)}) %reduce-scatter.11.cloned.1.call-update) | async-done | bytes 393232 | tf_op jit(solution)/shard_map/reduce_scatter | solution.py:102
  329.4 0.0 copy-done
  329.4 0.0 copy-done.3
  329.4 1.3 fusion.21
  330.6 16.2 %psum.62 = f32[1536]{0:T(1024)S(1)} all-reduce(f32[1536]{0:T(1024)S(1)} %get-tuple-element.6), channel_id=1, replica_groups=mesh['row'=8,'col'=4] {'row'}, use_global_device_ids=true, to_apply=%region_19.20 | all-reduce | flops 1536 | bytes 12288 | tf_op jit(solution)/shard_map/psum | solution.py:114
  346.8 0.6 multiply_reduce_fusion.3
  348.1 38.5 %psum.63 = f32[]{:T(128)} all-reduce(f32[]{:T(128)S(6)} %add.76), channel_id=1, replica_groups=mesh['row'=8,'col'=4] {'row','col'}, use_global_device_ids=true, to_apply=%region_21.22 | all-reduce | flops 1 | bytes 8 | tf_op jit(solution)/shard_map/psum | solution.py:116
  387.3 10.1 %all-reduce = (f32[64]{0:T(128)S(1)}, f32[64]{0:T(128)S(1)}) all-reduce(f32[64]{0:T(128)S(1)} %get-tuple-element.7, f32[64]{0:T(128)S(1)} %get-tuple-element.8), channel_id=1, replica_groups=mesh['row'=8,'col'=4] {'col'}, use_global_device_ids=true, to_apply=%region_15.16 | all-reduce | flops 128 | bytes 1024 | tf_op jit(solution)/shard_map/psum | solution.py:106
  397.5 0.6 broadcast_multiply_fusion.2
  398.1 0.0 copy-done.2
  398.1 2.0 fusion.20
  400.1 8.7 %broadcast_multiply_fusion = f32[1536,1536]{1,0:T(8,128)} fusion(f32[1536,1536]{1,0:T(8,128)} %get-tuple-element.31, f32[]{:T(128)S(6)} %min.3), kind=kLoop, calls=%fused_computation.3 | loop fusion | flops 2359296 | bytes 18874372 | tf_op jit(solution)/shard_map/mul | solution.py:121
  408.8 0.0 slice-done
  408.8 0.0 slice-done.1
  408.8 0.0 copy-start.1
  408.8 4.8 %broadcast_multiply_fusion.1 = f32[1536,1536]{1,0:T(8,128)} fusion(f32[1536,1536]{1,0:T(8,128)S(1)} %bitcast.13, f32[]{:T(128)S(6)} %min.3), kind=kLoop, calls=%fused_computation.4 | loop fusion | flops 2359296 | bytes 18874372 | tf_op jit(solution)/shard_map/mul | solution.py:121
  413.6 1.7 fusion.27
  (22 shorter events, 0.3 us)
Async XLA Ops:
  7.2 30.5 %all-gather.12.cloned.1.call-start = ((), (), s32[]{:S(2)}) async-start(), calls=%async_computation.9 | async-start | bytes 1769472 | tf_op jit(solution)/shard_map/all_gather | solution.py:92
  7.9 56.4 %all-gather.6.cloned.1.call-start = ((), (), s32[]{:S(2)}) async-start(), calls=%async_computation.4 | async-start | bytes 1769472 | tf_op jit(solution)/shard_map/all_gather | solution.py:55
  23.6 67.3 %all-gather.8.cloned.1.call-start = ((), (), s32[]{:S(2)}) async-start(), calls=%async_computation.5 | async-start | bytes 1769472 | tf_op jit(solution)/shard_map/all_gather | solution.py:56
  24.3 113.1 %reduce-scatter.9.cloned.1.call-start = ((), (), s32[]{:S(2)}) async-start(), calls=%async_computation.10 | async-start | bytes 3932160 | tf_op jit(solution)/shard_map/reduce_scatter | solution.py:93
  44.8 166.1 %reduce-scatter.5.cloned.1.call-start = ((), (), s32[]{:S(2)}) async-start(), calls=%async_computation.6 | async-start | bytes 7864320 | tf_op jit(solution)/shard_map/reduce_scatter | solution.py:59
  99.1 165.8 %all-gather.10.cloned.1.call-start = ((), (), s32[]{:S(2)}) async-start(), calls=%async_computation.7 | async-start | bytes 1966080 | tf_op jit(solution)/shard_map/all_gather | solution.py:85
  213.9 72.8 %all-gather.14.cloned.1.call-start = ((), (), s32[]{:S(2)}) async-start(), calls=%async_computation.12 | async-start | bytes 1966080 | tf_op jit(solution)/shard_map/all_gather | solution.py:97
  213.9 13.0 %collective-permute-start = (bf16[128,1536]{1,0:T(8,128)(2,1)S(1)}, bf16[128,1536]{1,0:T(8,128)(2,1)S(1)}, u32[]{:S(2)}, u32[]{:S(2)}) collective-permute-start(bf16[128,1536]{1,0:T(8,128)(2,1)S(1)} %get-tuple-element.20), channel_id=1, source_target_pairs={{0,1},{1,2},{2,3},{3,0},{4,5},{5,6},{6,7},{7,4},{8,9},{9,10},{10,1... | collective-permute-start | bytes 1179656 | tf_op jit(solution)/shard_map/ppermute | solution.py:17
  227.0 11.3 %collective-permute-start.1 = (bf16[128,1536]{1,0:T(8,128)(2,1)S(1)}, bf16[128,1536]{1,0:T(8,128)(2,1)S(1)}, u32[]{:S(2)}, u32[]{:S(2)}) collective-permute-start(bf16[128,1536]{1,0:T(8,128)(2,1)S(1)} %collective-permute-done), channel_id=1, source_target_pairs={{0,1},{1,2},{2,3},{3,0},{4,5},{5,6},{6,7},{7,4},{8,9},{9,10},{10,1... | collective-permute-start | bytes 1179656 | tf_op jit(solution)/shard_map/ppermute | solution.py:17
  238.2 17.8 %collective-permute-start.2 = (bf16[128,1536]{1,0:T(8,128)(2,1)S(1)}, bf16[128,1536]{1,0:T(8,128)(2,1)S(1)}, u32[]{:S(2)}, u32[]{:S(2)}) collective-permute-start(bf16[128,1536]{1,0:T(8,128)(2,1)S(1)} %collective-permute-done.1), channel_id=1, source_target_pairs={{0,1},{1,2},{2,3},{3,0},{4,5},{5,6},{6,7},{7,4},{8,9},{9,10},{10,1... | collective-permute-start | bytes 1179656 | tf_op jit(solution)/shard_map/ppermute | solution.py:17
  239.1 90.2 %reduce-scatter.11.cloned.1.call-start = ((), (), s32[]{:S(2)}) async-start(), calls=%async_computation.11 | async-start | bytes 3538944 | tf_op jit(solution)/shard_map/reduce_scatter | solution.py:102
  256.3 1.7 copy-start.4
  264.7 148.9 %reduce-scatter.7.cloned.1.call-start = ((), (), s32[]{:S(2)}) async-start(), calls=%async_computation.8 | async-start | bytes 3538944 | tf_op jit(solution)/shard_map/reduce_scatter | solution.py:89
  272.1 1.9 copy-start.5
  281.4 47.9 %copy-start = (bf16[64,1536]{1,0:T(8,128)(2,1)S(1)}, bf16[64,1536]{1,0:T(8,128)(2,1)}, u32[]{:S(2)}) copy-start(bf16[64,1536]{1,0:T(8,128)(2,1)} %param.7) | copy-start | bytes 589828
  281.4 47.9 %copy-start.3 = (f32[1536]{0:T(1024)S(1)}, f32[1536]{0:T(1024)}, u32[]{:S(2)}) copy-start(f32[1536]{0:T(1024)} %param.9) | copy-start | bytes 18436
  281.4 116.6 %copy-start.2 = (bf16[64,1536]{1,0:T(8,128)(2,1)S(1)}, bf16[64,1536]{1,0:T(8,128)(2,1)}, u32[]{:S(2)}) copy-start(bf16[64,1536]{1,0:T(8,128)(2,1)} %param.8) | copy-start | bytes 589828
  398.1 10.7 %slice-start = ((s8[9437184]{0:T(1024)(128)(4,1)}), s8[4194304]{0:T(1024)(128)(4,1)S(1)}, s32[]{:S(2)}) async-start(s8[9437184]{0:T(1024)(128)(4,1)} %bitcast.12), calls=%async_computation.13 | async-start | bytes 8388608
  400.1 8.7 %slice-start.1 = ((s8[9437184]{0:T(1024)(128)(4,1)}), s8[4194304]{0:T(1024)(128)(4,1)S(1)}, s32[]{:S(2)}) async-start(s8[9437184]{0:T(1024)(128)(4,1)} %bitcast.12), calls=%async_computation.14 | async-start | bytes 8388608
  400.1 8.7 %slice-start.2 = ((s8[9437184]{0:T(1024)(128)(4,1)}), s8[1048576]{0:T(1024)(128)(4,1)S(1)}, s32[]{:S(2)}) async-start(s8[9437184]{0:T(1024)(128)(4,1)} %bitcast.12), calls=%async_computation.15 | async-start | bytes 2097152
  408.8 4.8 %copy-start.1 = (bf16[64,1536]{1,0:T(8,128)(2,1)S(1)}, bf16[64,1536]{1,0:T(8,128)(2,1)}, u32[]{:S(2)}) copy-start(bf16[64,1536]{1,0:T(8,128)(2,1)} %param.6) | copy-start | bytes 589828
Sparse Core Ops, SparseCore 0:
  9.6 27.9 all-gather.11
  39.8 24.3 all-gather.5
  66.5 24.3 all-gather.7
  94.3 43.0 reduce-scatter.8
  140.8 70.0 reduce-scatter.4
  214.0 40.0 all-gather.9
  255.9 30.7 all-gather.13
  289.0 40.3 reduce-scatter.10
  331.7 39.8 reduce-scatter.6
